TPU v7x, 32 devices: a whole 2x2x4 slice. The times are simulated.
32 devices in a mesh: row: 8 (over z, y), col: 4 (over x, core).
Axes of the slice: x: 2, y: 2, z: 4, core: 2. Of those that a mesh axis runs over, the one named last changes fastest.
Arguments:
- eigvec: float32 [32, 8, 128, 1024], P(None, 'row', None, 'col'), may hold values from -6 to 6
- reflectors: float32 [2, 32, 8, 256, 128], P(None, None, 'row', 'col'), may hold values from -6 to 6
- sweep_group: int32 [2, 32, 8], P(None, None, 'row'), may hold values from -1 to 254, as said below
Outputs:
- transformed: float32 [32, 8, 128, 1024], P(None, 'row', None, 'col')
Inputs may be any that keep to these rules, and one draw needn't show every extreme that they name: `sweep_group`: -1 where no diamond sits at that diagonal and tile position (tile position l * R + r for entry [d, l, r]); otherwise the diamond's sweep group, at most its tile position. Within one diagonal no two diamonds sit at adjacent tile positions, and none sits at the last tile position 255.
All inputs are finite; a program needn't handle non-finite values.
Results may differ from a plain program's by a relative error of at most 0.0003.
Values sent between devices are 32-bit elements.
A program may use at most 128 MiB of HBM per device.

v0:
```python
import functools

import jax
import jax.numpy as jnp
from jax import lax
from jax.experimental import pallas as pl
from jax.experimental.pallas import tpu as pltpu
from jax.sharding import PartitionSpec as P

GROUP = 1
CHUNKS = 1
PROFILES = (
    (12, 4, 4, 12), (12, 5, 5, 12), (13, 5, 5, 13), (13, 5, 6, 14), (14, 6, 5, 13), (13, 5, 7, 15),
    (15, 7, 5, 13), (15, 7, 6, 14), (16, 5, 6, 17), (15, 7, 8, 15), (17, 8, 7, 16), (20, 12, 12, 20),
)
GROUPED = 8
SPARE = 10 * 2**20


def split(x):
    high = x.astype(jnp.bfloat16)
    return high, (x - high.astype(jnp.float32)).astype(jnp.bfloat16)


def dot(a, b):
    return jnp.dot(a, b, preferred_element_type=jnp.float32)


def dot3(a, b):
    return dot(a[1], b[0]) + dot(a[0], b[1]) + dot(a[0], b[0])


def bounds(slots):
    inner = [slots * i // CHUNKS // GROUP * GROUP for i in range(CHUNKS)]
    return inner + [slots]


def chunk_shapes(slots, tiles):
    edges = bounds(slots)
    return [
        jax.ShapeDtypeStruct((high - low,) + tiles.shape[1:], tiles.dtype)
        for low, high in zip(edges[:-1], edges[1:])
    ]


def slot_of(chunks, k):
    for chunk in chunks:
        if k < chunk.shape[0]:
            return chunk.at[k]
        k -= chunk.shape[0]


def gather_kernel(slots, own, behind, panels, tiles, picked, *rest):
    diagonals = panels.shape[0]
    sent, sems = rest[:-1], rest[-1]

    def panel_copy(d, k):
        return pltpu.make_async_copy(
            panels.at[d, own[d, k]], picked.at[d, k], sems.at[d * slots + k]
        )

    def tile_copy(k):
        return pltpu.make_async_copy(
            tiles.at[behind[0, k]], slot_of(sent, k), sems.at[diagonals * slots + k]
        )

    for k in range(slots):
        tile_copy(k).start()
    for d in range(diagonals):
        for k in range(slots):
            panel_copy(d, k).start()
    for k in range(slots):
        tile_copy(k).wait()
    for d in range(diagonals):
        for k in range(slots):
            panel_copy(d, k).wait()


def gather(slots, own, behind, panels, tiles):
    diagonals = panels.shape[0]
    any_spec = pl.BlockSpec(memory_space=pl.ANY)
    return pl.pallas_call(
        functools.partial(gather_kernel, slots),
        grid_spec=pltpu.PrefetchScalarGridSpec(
            num_scalar_prefetch=2,
            grid=(1,),
            in_specs=[any_spec, any_spec],
            out_specs=[pl.BlockSpec(memory_space=pltpu.VMEM)] * (1 + CHUNKS),
            scratch_shapes=[pltpu.SemaphoreType.DMA(((diagonals + 1) * slots,))],
        ),
        out_shape=[
            jax.ShapeDtypeStruct((diagonals, slots) + panels.shape[2:], panels.dtype),
        ] + chunk_shapes(slots, tiles),
        name="gather",
    )(own, behind, panels, tiles)


def scatter_kernel(slots, diagonal, more, behind, counts, tiles, *rest):
    returned, out, sent, sems = rest[:CHUNKS], rest[CHUNKS], rest[CHUNKS + 1:-1], rest[-1]

    def put(k):
        return pltpu.make_async_copy(
            slot_of(returned, k), out.at[behind[diagonal, k]], sems.at[k]
        )

    for k in range(slots):
        @pl.when(k < counts[1, diagonal])
        def _():
            put(k).start()
    for k in range(slots):
        @pl.when(k < counts[1, diagonal])
        def _():
            put(k).wait()
    if more:

        def take(k):
            return pltpu.make_async_copy(
                out.at[behind[diagonal + 1, k]], slot_of(sent, k), sems.at[slots + k]
            )

        for k in range(slots):
            take(k).start()
        for k in range(slots):
            take(k).wait()


def scatter(slots, diagonal, more, behind, counts, tiles, returned):
    any_spec = pl.BlockSpec(memory_space=pl.ANY)
    vmem_spec = pl.BlockSpec(memory_space=pltpu.VMEM)
    shapes = [jax.ShapeDtypeStruct(tiles.shape, tiles.dtype)]
    if more:
        shapes += chunk_shapes(slots, tiles)
    return pl.pallas_call(
        functools.partial(scatter_kernel, slots, diagonal, more),
        grid_spec=pltpu.PrefetchScalarGridSpec(
            num_scalar_prefetch=2,
            grid=(1,),
            in_specs=[any_spec] + [vmem_spec] * CHUNKS,
            out_specs=[any_spec] + [vmem_spec] * (len(shapes) - 1),
            scratch_shapes=[pltpu.SemaphoreType.DMA((2 * slots,))],
        ),
        out_shape=shapes,
        input_output_aliases={2: 0},
        name="scatter",
    )(behind, counts, tiles, *returned)


def factor_kernel(pieces_count, col_ref, *refs):
    pieces = refs[:pieces_count]
    vh_ref, vl_ref, yh_ref, yl_ref = refs[pieces_count:]
    me = col_ref[0]
    group = pieces[0].shape[1]
    band = pieces[0].shape[-1]
    depth = pieces_count * pieces[0].shape[2]
    row = lax.broadcasted_iota(jnp.int32, (depth, band), 0)
    col = lax.broadcasted_iota(jnp.int32, (depth, band), 1)
    inside = (row >= col + 1) & (row <= col + band)
    leading = row == col + 1
    r = lax.broadcasted_iota(jnp.int32, (band, band), 0)
    c = lax.broadcasted_iota(jnp.int32, (band, band), 1)
    slots = range(group)
    vs, ts, factors, inverses = [], [], [], []
    for g in slots:
        parts = [piece[0, g] for piece in pieces]
        stride = 1
        while stride < pieces_count:
            odd = (me // stride) % 2 == 1
            parts = [
                jnp.where(odd, parts[j ^ stride], parts[j]) for j in range(pieces_count)
            ]
            stride *= 2
        panel = jnp.concatenate(parts, axis=0)
        v = jnp.where(leading, 1.0, jnp.where(inside, panel, 0.0))
        vs.append(split(v))
        ts.append(split(v.T))
        vh_ref[g] = vs[g][0]
        vl_ref[g] = vs[g][1]
    for g in slots:
        gram = dot3(ts[g], vs[g])
        diagonal = jnp.sum(jnp.where(r == c, gram, 0.0), axis=0, keepdims=True)
        factors.append(gram)
        inverses.append(jnp.where(r == c, 2.0 / diagonal, 0.0))

    def level(n, inverses):
        coupling = ((r >> n) != (c >> n)) & ((r >> (n + 1)) == (c >> (n + 1))) & (r < c)
        inverse_parts = [split(inverse) for inverse in inverses]
        middles = [
            split(dot3(split(jnp.where(coupling, factors[g], 0.0)), inverse_parts[g]))
            for g in slots
        ]
        return tuple(inverses[g] - dot3(inverse_parts[g], middles[g]) for g in slots)

    inverses = lax.fori_loop(0, (band - 1).bit_length(), level, tuple(inverses))
    for g in slots:
        high, low = split(dot3(split(inverses[g]), ts[g]))
        yh_ref[g] = high
        yl_ref[g] = low


def factor(first, slots, diagonal, col, pieces):
    count = len(pieces)
    _, _, height, band = pieces[0].shape
    depth = count * height
    group = GROUP if slots % GROUP == 0 else 1
    start = first // group
    kind = jnp.bfloat16
    return pl.pallas_call(
        functools.partial(factor_kernel, count),
        grid_spec=pltpu.PrefetchScalarGridSpec(
            num_scalar_prefetch=1,
            grid=(slots // group,),
            in_specs=[
                pl.BlockSpec((1, group, height, band), lambda k, c: (diagonal, k + start, 0, 0))
            ] * count,
            out_specs=[pl.BlockSpec((group, depth, band), lambda k, c: (k, 0, 0))] * 2
            + [pl.BlockSpec((group, band, depth), lambda k, c: (k, 0, 0))] * 2,
        ),
        out_shape=[jax.ShapeDtypeStruct((slots, depth, band), kind)] * 2
        + [jax.ShapeDtypeStruct((slots, band, depth), kind)] * 2,
        name="factor",
    )(col, *pieces)


def apply_kernel(diagonal, first, own, counts, tile, below, vh, vl, yh, yl, tile_out, below_out):
    k = pl.program_id(0) + first
    band = tile.shape[1]
    upper, lower = tile[0], below[0]
    stacked = jnp.concatenate([upper, lower], axis=0)
    solved = dot3((yh[0], yl[0]), split(stacked))
    change = dot3((vh[0], vl[0]), split(solved))
    active = k < counts[0, diagonal]
    tile_out[0] = jnp.where(active, upper - change[:band], upper)
    below_out[0] = jnp.where(active, lower - change[band:], lower)


def apply(first, diagonal, own, counts, tiles, beneath, vh, vl, yh, yl):
    _, band, columns = tiles.shape
    depth = vh.shape[1]
    at_slot = lambda k, own, counts: (k, 0, 0)
    at_own = lambda k, own, counts: (own[diagonal, k + first], 0, 0)
    return pl.pallas_call(
        functools.partial(apply_kernel, diagonal, first),
        grid_spec=pltpu.PrefetchScalarGridSpec(
            num_scalar_prefetch=2,
            grid=(beneath.shape[0],),
            in_specs=[
                pl.BlockSpec((1, band, columns), at_own),
                pl.BlockSpec((1, band, columns), at_slot),
                pl.BlockSpec((1, depth, band), at_slot),
                pl.BlockSpec((1, depth, band), at_slot),
                pl.BlockSpec((1, band, depth), at_slot),
                pl.BlockSpec((1, band, depth), at_slot),
            ],
            out_specs=[
                pl.BlockSpec((1, band, columns), at_own),
                pl.BlockSpec((1, band, columns), at_slot),
            ],
        ),
        out_shape=[
            jax.ShapeDtypeStruct(tiles.shape, tiles.dtype),
            jax.ShapeDtypeStruct(beneath.shape, beneath.dtype),
        ],
        input_output_aliases={2: 0},
        name="apply",
    )(own, counts, tiles, beneath, vh, vl, yh, yl)


def lift(sent, to_above):
    beneath = []
    for chunk in sent:
        beneath.append(lax.ppermute(chunk, "row", to_above))
    return beneath


def steps(slots, own, behind, counts, tiles, panels):
    row_count = lax.axis_size("row")
    col_count = lax.axis_size("col")
    col = lax.axis_index("col").astype(jnp.int32)[None]
    diagonals = panels.shape[0]
    to_above = [(i, (i - 1) % row_count) for i in range(row_count)]
    to_below = [(i, (i + 1) % row_count) for i in range(row_count)]
    picked, *sent = gather(slots, own, behind, panels, tiles)
    beneath = lift(sent, to_above)
    pieces = {0: picked}
    stride = col_count // 2
    while stride >= 1:
        swap = [(i, i ^ stride) for i in range(col_count)]
        pieces.update(
            {q ^ stride: lax.ppermute(p, "col", swap) for q, p in pieces.items()}
        )
        stride //= 2
    pieces = [pieces[q] for q in range(col_count)]
    for diagonal in range(diagonals):
        returned = []
        for first, chunk in zip(bounds(slots), beneath):
            factors = factor(first, chunk.shape[0], diagonal, col, pieces)
            tiles, lower = apply(first, diagonal, own, counts, tiles, chunk, *factors)
            returned.append(lax.ppermute(lower, "row", to_below))
        more = diagonal + 1 < diagonals
        tiles, *sent = scatter(slots, diagonal, more, behind, counts, tiles, returned)
        if more:
            beneath = lift(sent, to_above)
    return tiles


def plan_kernel(profiles, flags, table, choice, everyone, mine, held, send, recv):
    count, _, lanes = held.shape
    diagonals, depth = flags.shape
    me = lax.axis_index("row")
    mine[...] = jnp.full(mine.shape, -1, mine.dtype)
    mine[0:diagonals, 0:depth] = flags[...]
    barrier = pltpu.get_barrier_semaphore()
    mesh_id = pl.DeviceIdType.MESH
    others = [lax.rem(me + by, count) for by in range(1, count)]
    for other in others:
        pl.semaphore_signal(
            barrier, inc=1, device_id={"row": other}, device_id_type=mesh_id
        )
    pl.semaphore_wait(barrier, count - 1)
    copies = [
        pltpu.make_async_remote_copy(
            src_ref=mine,
            dst_ref=held.at[me],
            send_sem=send.at[i],
            recv_sem=recv.at[i],
            device_id={"row": other},
            device_id_type=mesh_id,
        )
        for i, other in enumerate(others)
    ]
    for copy in copies:
        copy.start()
    held[me] = mine[...]
    for copy in copies:
        copy.wait()
    everyone[...] = held[...]

    f32 = jnp.float32
    row = lax.broadcasted_iota(jnp.int32, (count, lanes), 0)
    on = [jnp.where(held[:, d, :] >= 0, 1.0, 0.0) for d in range(2)]
    after = []
    for x in on:
        under = pltpu.roll(x, count - 1, axis=0)
        after.append(jnp.where(row == count - 1, pltpu.roll(under, lanes - 1, axis=1), under))
    again = on[0] * on[1]
    first, second = on[0] - again, on[1] - again
    kinds = [
        first * after[1],
        first - first * after[1],
        again,
        second - second * after[0],
        second * after[0],
    ]
    sums = [jnp.sum(x, axis=1, keepdims=True) for x in kinds]
    must, may, rep, ready, unready = sums
    chosen = [jnp.zeros((1, 1), f32) for _ in range(4)]
    index, missed = jnp.zeros((1, 1), f32), jnp.ones((1, 1), f32)
    for early, soon, late, last in profiles:
        bad = (must + may + rep > early) | (must > soon)
        bad |= rep + ready + unready + jnp.maximum(must + may - soon, 0.0) > last
        bad |= unready + jnp.maximum(ready - (early - must - may - rep), 0.0) > late
        still = missed * jnp.max(jnp.where(bad, 1.0, 0.0), axis=0, keepdims=True)
        for i, size in enumerate((early, soon, late, last)):
            chosen[i] = chosen[i] + (missed - still) * size
        index, missed = index + still, still
    choice[0] = index[0, 0].astype(jnp.int32)
    early, soon, late, last = chosen

    above = lax.rem(me + count - 1, count)
    picked = [
        jnp.sum(jnp.where(row == who, x, 0.0), axis=0, keepdims=True)
        for who in (me, above)
        for x in kinds
    ]
    none = jnp.zeros((1, lanes), f32)
    stacked = jnp.concatenate(picked + [none] * 6, axis=0)
    r = lax.broadcasted_iota(jnp.int32, (lanes, lanes), 0)
    c = lax.broadcasted_iota(jnp.int32, (lanes, lanes), 1)
    ahead = jnp.dot(
        stacked.astype(jnp.bfloat16),
        jnp.where(r < c, 1.0, 0.0).astype(jnp.bfloat16),
        preferred_element_type=f32,
    )
    totals = jnp.sum(stacked, axis=1, keepdims=True)

    def places(which):
        at = [stacked[5 * which + i : 5 * which + i + 1] > 0.5 for i in range(5)]
        rank = [ahead[5 * which + i : 5 * which + i + 1] for i in range(5)]
        must, may, rep, ready, unready = [
            totals[5 * which + i : 5 * which + i + 1] for i in range(5)
        ]
        slot0 = jnp.where(
            at[0],
            rank[0],
            jnp.where(at[1], must + rank[1], jnp.where(at[2], must + may + rank[2], -1.0)),
        )
        taken = must + may + rep
        spare = early - taken
        over = jnp.maximum(ready - spare, 0.0)
        tardy = over + unready
        prompt = rep + ready - over

        def placed(p):
            return jnp.where(p < last - late, p, p + tardy)

        fast = at[3] & (rank[3] < spare)
        lag = jnp.where(
            at[4], over + rank[4], jnp.where(at[3] & ~fast, rank[3] - spare, -1.0)
        )
        slot1 = jnp.where(
            at[2],
            placed(rank[2]),
            jnp.where(fast, placed(rep + rank[3]), jnp.where(lag >= 0, last - late + lag, -1.0)),
        )
        single = at[0] | at[1]
        held_back = single & (slot0 >= soon)
        kept = jnp.where(held_back, placed(prompt + slot0 - soon), -1.0)
        sooner = jnp.where(single & (slot0 < soon), slot0, -1.0)
        ahead_of = jnp.where(fast, taken + rank[3], -1.0)
        return at, slot0, slot1, kept, sooner, ahead_of, lag

    top = me == 0

    def below(x):
        return jnp.where(top, pltpu.roll(x, 1, axis=1), x)

    at, slot0, slot1, kept, _, ahead_of, _ = places(0)
    _, up0, up1, up_kept, up_sooner, up_ahead, up_lag = places(1)
    keys = [
        slot0,
        slot1,
        kept,
        jnp.maximum(up0, up_ahead),
        up_lag,
        jnp.where(at[2], slot0, -1.0),
        ahead_of,
        below(up_sooner),
    ]
    filler = jnp.zeros((lanes - len(keys), lanes), f32)
    turned = jnp.concatenate(keys + [filler], axis=0).T
    column = lambda i: turned[:, i : i + 1]
    tile = r.astype(f32)
    place = c.astype(f32)

    def turn(key, value, missing):
        hit = jnp.where(column(key) == place, value - missing, 0.0)
        return jnp.sum(hit, axis=0, keepdims=True) + missing


    def behind(key):
        found = turn(key, tile, 0.0)
        return jnp.where(top, jnp.minimum(found + 1.0, depth - 1.0), found)

    owned = [turn(0, tile, 0.0), turn(1, tile, 0.0)]
    rows = [
        owned[0],
        owned[1],
        behind(3),
        behind(4),
        slot0,
        jnp.where(slot1 >= 0, slot1 + early, -1.0),
        below(up_sooner),
        below(jnp.maximum(up1, up_kept)),
        turn(1, column(5), -1.0),
        turn(1, column(7), -1.0),
        turn(1, column(6), -1.0),
        owned[0],
        owned[1],
        turn(2, column(0), -1.0),
    ]
    rows += [none] * (table.shape[0] - len(rows))
    table[...] = jnp.concatenate(rows, axis=0).astype(jnp.int32)


def plan(profiles, flags):
    count = lax.axis_size("row")
    lanes = 128
    vmem_spec = pl.BlockSpec(memory_space=pltpu.VMEM)
    shape = (count, 8, lanes)
    kind = flags.dtype
    return pl.pallas_call(
        functools.partial(plan_kernel, profiles),
        out_shape=[
            jax.ShapeDtypeStruct((16, lanes), kind),
            jax.ShapeDtypeStruct((1,), kind),
            jax.ShapeDtypeStruct(shape, kind),
        ],
        in_specs=[vmem_spec],
        out_specs=[vmem_spec, pl.BlockSpec(memory_space=pltpu.SMEM), vmem_spec],
        scratch_shapes=[
            pltpu.VMEM(shape[1:], kind),
            pltpu.VMEM(shape, kind),
            pltpu.SemaphoreType.DMA((count - 1,)),
            pltpu.SemaphoreType.DMA((count - 1,)),
        ],
        compiler_params=pltpu.CompilerParams(collective_id=0, has_side_effects=True),
        name="plan",
    )(flags)


def fresh_kernel(x, out):
    out[...] = x[...]


def fresh(x):
    spec = pl.BlockSpec((1,) + x.shape[1:], lambda k: (k, 0, 0))
    return pl.pallas_call(
        fresh_kernel,
        grid=(x.shape[0],),
        in_specs=[spec],
        out_specs=spec,
        out_shape=jax.ShapeDtypeStruct(x.shape, x.dtype),
        name="fresh",
    )(x)


def ordering(active):
    depth = active.shape[-1]
    here = jnp.arange(depth, dtype=jnp.int32)
    on = active.astype(jnp.int32)
    earlier = here[None, :] < here[:, None]
    before = jnp.sum(jnp.where(earlier, on[..., None, :], 0), axis=-1)
    total = jnp.sum(on, axis=-1)
    rank = jnp.where(active, before, total[..., None] + here - before)
    order = jnp.sum(
        jnp.where(rank[..., None, :] == here[:, None], here, 0), axis=-1
    ).astype(jnp.int32)
    return order, total.astype(jnp.int32)


def flipped(index, stride):
    return index + stride - 2 * stride * lax.rem(lax.div(index, stride), 2)


def wide(parts, axis):
    return jnp.concatenate(parts, axis=axis)


def square(a, b):
    size = b[0].shape[1]
    both = wide(b, 1)
    product = dot(wide(a, 1), wide([both, both], 0))
    return product[:, :size] + product[:, size:]


def invert_and_store(panels, first, count, vh_ref, vl_ref, yh_ref, yl_ref):
    depth, band = panels.shape[1:]
    row = lax.broadcasted_iota(jnp.int32, (depth, band), 0)
    col = lax.broadcasted_iota(jnp.int32, (depth, band), 1)
    inside = (row >= col + 1) & (row <= col + band)
    leading = row == col + 1
    r = lax.broadcasted_iota(jnp.int32, (band, band), 0)
    c = lax.broadcasted_iota(jnp.int32, (band, band), 1)
    slots = range(count)
    ts, factors, inverses = [], [], []
    for g in slots:
        v = jnp.where(leading, 1.0, jnp.where(inside, panels[first + g], 0.0))
        vs = split(v)
        ts.append(split(v.T))
        vh_ref[first + g] = vs[0]
        vl_ref[first + g] = vs[1]
        product = dot(wide(ts[g], 0), wide(vs, 1))
        gram = product[:band, :band] + (product[:band, band:] + product[band:, :band])
        diagonal = jnp.sum(jnp.where(r == c, gram, 0.0), axis=0, keepdims=True)
        factors.append(jnp.where(r < c, gram, 0.0))
        inverses.append(jnp.where(r == c, 2.0 / diagonal, 0.0))

    def level(n, inverses):
        coupling = ((r >> n) != (c >> n)) & ((r >> (n + 1)) == (c >> (n + 1)))
        inverse_parts = [split(inverse) for inverse in inverses]
        middles = [
            split(square(split(jnp.where(coupling, factors[g], 0.0)), inverse_parts[g]))
            for g in slots
        ]
        return tuple(inverses[g] - square(inverse_parts[g], middles[g]) for g in slots)

    inverses = lax.fori_loop(0, (band - 1).bit_length(), level, tuple(inverses))
    for g in slots:
        parts = split(inverses[g])
        high, low = ts[g]
        product = dot(wide(parts, 1), wide([high, high], 0)) + dot(parts[0], low)
        yh_ref[first + g], yl_ref[first + g] = split(product)


def whole_kernel(
    profile, group, table, tiles_in, panels_in, merged, last_back,
    tiles, pieces, panel, vh, vl, yh, yl, lift_out, lift_in, upper_new, lower_new, first_back,
    upper_now, lower_now, in_sems, panel_sems, lift_sems, back_sems,
):
    early, soon, late, last = profile
    slots, lifts, backs = (early, last), (early, late), (soon, last)
    skip = (0, last - late)
    groups = [-(-n // group) for n in slots]
    depth = tiles.shape[0]
    height = pieces.shape[2]
    rows = lax.axis_size("row")
    cols = lax.axis_size("col")
    me_row = lax.axis_index("row")
    me_col = lax.axis_index("col")
    above = lax.rem(me_row + rows - 1, rows)
    below = lax.rem(me_row + 1, rows)
    mesh_id = pl.DeviceIdType.MESH
    strides = []
    stride = cols // 2
    while stride >= 1:
        strides.append(stride)
        stride //= 2

    def by(d, pair):
        return pair[0] + d * (pair[1] - pair[0])

    def either(source, index, other):
        return jnp.where(index >= 0, source[jnp.maximum(index, 0)], other)

    panels_copy = pltpu.make_async_copy(panels_in, pieces, in_sems.at[0])
    tiles_copy = pltpu.make_async_copy(tiles_in, tiles, in_sems.at[1])
    panels_copy.start()
    tiles_copy.start()

    barrier = pltpu.get_barrier_semaphore()
    peers = [{"row": above}, {"row": below}]
    peers += [{"col": flipped(me_col, s)} for s in strides]
    for peer in peers:
        pl.semaphore_signal(barrier, inc=1, device_id=peer, device_id_type=mesh_id)
    pl.semaphore_wait(barrier, len(peers))

    def exchange(g, stage):
        held = [me_col]
        for s in strides[:stage]:
            held += [flipped(h, s) for h in held]
        base = sum(2**i for i in range(stage))
        copies = []
        for i, h in enumerate(held):
            where = (pl.ds(g * group, group), pl.ds(pl.multiple_of(h * height, height), height))
            copies.append(
                pltpu.make_async_remote_copy(
                    src_ref=panel.at[where],
                    dst_ref=panel.at[where],
                    send_sem=panel_sems.at[0, g, base + i],
                    recv_sem=panel_sems.at[1, g, base + i],
                    device_id={"col": flipped(me_col, strides[stage])},
                    device_id_type=mesh_id,
                )
            )
        return copies

    def lift(d, k):
        return pltpu.make_async_remote_copy(
            src_ref=lift_out.at[d * early + k],
            dst_ref=lift_in[d].at[skip[d] + k],
            send_sem=lift_sems.at[0, d * early + k],
            recv_sem=lift_sems.at[1, d * early + k],
            device_id={"row": above},
            device_id_type=mesh_id,
        )

    def give_back(d, k):
        return pltpu.make_async_remote_copy(
            src_ref=lower_new.at[d * early + k],
            dst_ref=(first_back, last_back)[d].at[k],
            send_sem=back_sems.at[0, d * soon + k],
            recv_sem=back_sems.at[1, d * soon + k],
            device_id={"row": below},
            device_id_type=mesh_id,
        )

    def repeat(count, body):
        def one(k, _):
            body(k)
            return 0

        lax.fori_loop(0, count, one, 0)

    mine = pl.ds(pl.multiple_of(me_col * height, height), height)

    def pick_panels(d):
        def one(g):
            for i in range(group):
                at = g * group + i
                panel[d * groups[0] * group + at, mine] = pieces[d, table[11 + d, at]]
            if strides:
                for copy in exchange(d * groups[0] + g, 0):
                    copy.start()

        repeat(groups[d], one)

    def forward(g):
        for stage in range(1, len(strides)):
            for copy in exchange(g, stage - 1):
                copy.wait_recv()
            for copy in exchange(g, stage):
                copy.start()

    def factor(d):
        count = by(d, groups)

        def one(at):
            g = d * groups[0] + at
            if strides:
                for copy in exchange(g, len(strides) - 1):
                    copy.wait_recv()

            @pl.when(at + 1 < count)
            def _():
                forward(g + 1)

            invert_and_store(panel, g * group, group, vh, vl, yh, yl)

        forward(d * groups[0])
        repeat(count, one)

    def send_lifts(d, value):
        def one(k):
            lift_out[d * early + k] = value(table[2 + d, k])

            @pl.when(k > 0)
            def _():
                lift(d, k - 1).start()

        repeat(lifts[d], one)
        lift(d, lifts[d] - 1).start()

    def reflect(d):
        def one(k):
            slot = d * early + k
            at = d * groups[0] * group + k

            @pl.when(d == 0)
            def _():
                lift(0, k).wait_recv()
                upper_now[...] = tiles[table[0, k]]
                lower_now[...] = lift_in[0][k]

            @pl.when(d == 1)
            def _():
                @pl.when(k >= skip[1])
                def _():
                    lift(1, k - skip[1]).wait_recv()

                kept = either(first_back, table[9, k], tiles[table[1, k]])
                again = table[8, k]
                upper_now[...] = either(upper_new, again, kept)
                arrived = either(lift_in[0], table[10, k], lift_in[1][k])
                lower_now[...] = either(lower_new, again, arrived)

            upper, lower = upper_now[...], lower_now[...]
            band = upper.shape[0]
            stacked = split(jnp.concatenate([upper, lower], axis=0))
            solved = split(dot3((yh[at], yl[at]), stacked))
            change = dot3((vh[at], vl[at]), solved)
            lower_now[...] = lower - change[band:]
            upper_new[slot] = upper - change[:band]

            @pl.when(d == 0)
            def _():
                lower_new[slot] = lower_now[...]

                @pl.when(k < soon)
                def _():
                    give_back(0, k).start()

            @pl.when(d == 1)
            def _():
                lower_new[slot] = either(lower_new, table[13, k], lower_now[...])
                give_back(1, k).start()

        repeat(by(d, slots), one)

    def receive(d):
        repeat(backs[d], lambda k: give_back(d, k).wait_recv())

    panels_copy.wait()
    pick_panels(0)
    tiles_copy.wait()
    send_lifts(0, lambda j: tiles[j])
    pick_panels(1)

    def diagonal(d):
        factor(d)

        @pl.when(d == 1)
        def _():
            receive(0)

        reflect(d)

        @pl.when(d == 0)
        def _():
            send_lifts(1, lambda j: either(upper_new, table[4, j], tiles[j]))

    repeat(2, diagonal)

    def merge(j):
        kept = either(first_back, table[6, j], tiles[j])
        merged[j] = either(upper_new, table[5, j], either(upper_new, table[4, j], kept))

    repeat(depth, merge)
    receive(1)

    def drain(g):
        for stage in range(len(strides)):
            for copy in exchange(g, stage):
                copy.wait_send()

    repeat(sum(groups), drain)
    for d in range(2):
        repeat(lifts[d], lambda k, d=d: lift(d, k).wait_send())
        repeat(backs[d], lambda k, d=d: give_back(d, k).wait_send())


def settle_kernel(table, merged, back, out, sems):
    depth = merged.shape[0]

    def one(j, _):
        slot = table[7, j]

        @pl.when(slot >= 0)
        def _():
            pltpu.make_async_copy(back.at[jnp.maximum(slot, 0)], out.at[j], sems.at[j]).start()

        @pl.when(slot < 0)
        def _():
            pltpu.make_async_copy(merged.at[j], out.at[j], sems.at[j]).start()

        return 0

    def drain(j, _):
        pltpu.make_async_copy(merged.at[j], out.at[j], sems.at[j]).wait()
        return 0

    lax.fori_loop(0, depth, one, 0)
    lax.fori_loop(0, depth, drain, 0)


def settle(table, merged, back):
    vmem_spec = pl.BlockSpec(memory_space=pltpu.VMEM)
    return pl.pallas_call(
        settle_kernel,
        in_specs=[pl.BlockSpec(memory_space=pltpu.SMEM), vmem_spec, vmem_spec],
        out_specs=pl.BlockSpec(memory_space=pl.ANY),
        out_shape=jax.ShapeDtypeStruct(merged.shape, merged.dtype),
        scratch_shapes=[pltpu.SemaphoreType.DMA((merged.shape[0],))],
        compiler_params=pltpu.CompilerParams(vmem_limit_bytes=8 * 2**20),
        name="settle",
    )(table, merged, back)


def whole(profile, index, table, tiles, panels):
    depth, band, columns = tiles.shape
    _, _, height, _ = panels.shape
    cols = lax.axis_size("col")
    long = height * cols
    early, soon, late, last = profile
    group = GROUPED
    groups = [-(-n // group) for n in (early, last)]
    padded = sum(groups) * group
    f32, bf16 = jnp.float32, jnp.bfloat16
    tile_slots = lambda n: pltpu.VMEM((n, band, columns), f32)
    dma = pltpu.SemaphoreType.DMA
    scratch = [
        pltpu.VMEM(tiles.shape, f32),
        pltpu.VMEM(panels.shape, f32),
        pltpu.VMEM((padded, long, band), f32),
        pltpu.VMEM((padded, long, band), bf16),
        pltpu.VMEM((padded, long, band), bf16),
        pltpu.VMEM((padded, band, long), bf16),
        pltpu.VMEM((padded, band, long), bf16),
        tile_slots(early + late),
        [tile_slots(early), tile_slots(last)],
        tile_slots(early + last),
        tile_slots(early + last),
        tile_slots(soon),
        pltpu.VMEM((band, columns), f32),
        pltpu.VMEM((band, columns), f32),
        dma((2,)),
        dma((2, sum(groups), max(cols - 1, 1))),
        dma((2, early + late)),
        dma((2, soon + last)),
    ]
    tile_bytes = band * columns * 4
    held = 2 * depth + soon + late + 4 * early + 4 * last
    limit = held * tile_bytes + panels.size * 4 + padded * long * band * 12 + SPARE
    any_spec = pl.BlockSpec(memory_space=pl.ANY)
    vmem_spec = pl.BlockSpec(memory_space=pltpu.VMEM)
    merged, back = pl.pallas_call(
        functools.partial(whole_kernel, profile, group),
        in_specs=[pl.BlockSpec(memory_space=pltpu.SMEM), any_spec, any_spec],
        out_specs=[vmem_spec] * 2,
        out_shape=[
            jax.ShapeDtypeStruct(tiles.shape, f32),
            jax.ShapeDtypeStruct((last, band, columns), f32),
        ],
        scratch_shapes=scratch,
        compiler_params=pltpu.CompilerParams(
            collective_id=1 + index, has_side_effects=True, vmem_limit_bytes=limit
        ),
    )(table, tiles, panels)
    return settle(table, merged, back)


def local(eigvec, reflectors, sweep_group):
    row_index = lax.axis_index("row")
    row_count = lax.axis_size("row")
    depth = eigvec.shape[0]
    profiles = [p for p in PROFILES if max(p) <= depth]
    small = depth <= max(PROFILES[-1])
    if small and (depth,) * 4 not in profiles:
        profiles.append((depth,) * 4)
    table, choice, flags = plan(profiles, sweep_group[:, :, 0])

    def general(table, flags, tiles, panels):
        active = flags[:, : sweep_group.shape[0], :depth] >= 0
        mine = lax.dynamic_index_in_dim(active, row_index, 0, keepdims=False)
        above = lax.dynamic_index_in_dim(
            active, (row_index + row_count - 1) % row_count, 0, keepdims=False
        )
        order, counts = ordering(jnp.stack([mine, above]))
        own = order[0]
        behind = jnp.where(row_index == 0, (order[1] + 1) % depth, order[1])
        return steps(depth, own, behind, counts, fresh(tiles), panels)

    def branch(index, profile):
        return lambda table, flags, tiles, panels: whole(profile, index, table, tiles, panels)

    branches = [branch(i, p) for i, p in enumerate(profiles)]
    if not small:
        branches.append(general)
    args = (table, flags, eigvec[:, 0], reflectors[:, :, 0])
    out = lax.switch(choice[0], branches, *args) if len(branches) > 1 else branches[0](*args)
    return out[:, None]


def solution(mesh):
    return jax.shard_map(
        local,
        mesh=mesh,
        in_specs=(
            P(None, "row", None, "col"),
            P(None, None, "row", "col", None),
            P(None, None, "row"),
        ),
        out_specs=P(None, "row", None, "col"),
        check_vma=False,
    )
```

profile of v0, /device:TPU:0, one launch (start us, length us, event | category | flops | bytes accessed | tf_op | source)
XLA Modules:
  0.0 141.7 jit_solution(16424577863941880853)
XLA Ops:
  0.0 9.9 %plan.1 = (s32[16,128]{1,0:T(8,128)S(1)}, s32[1]{0:T(128)}, s32[8,8,128]{2,1,0:T(8,128)S(1)}) custom-call(s32[2,32]{1,0:T(2,128)} %bitcast.76), custom_call_target="tpu_custom_call" | custom-call | tf_op jit(solution)/shard_map/plan/pallas_call | solution.py:481
  10.5 130.9 %conditional.1 = (f32[32,1,128,256]{3,2,1,0:T(8,128)}) conditional(s32[]{:T(128)} %bitcast.43, (s32[16,128]{1,0:T(8,128)S(1)}, f32[32,128,256]{2,1,0:T(8,128)}, f32[2,32,64,128]{3,2,1,0:T(8,128)}) %tuple.112, (s32[16,128]{1,0:T(8,128)S(1)}, f32[32,128,256]{2,1,0:T(8,128)}, f32[2,32,64,128]{3,2,1,0:T(8,128)}) %tuple.113, ...), branch_computations={%region_0.0_spmd, %region_1.0_spmd, %region_2.0_spmd, %region_3.0_... | conditional | flops 23761 | bytes 109062456 | solution.py:929
  10.8 127.4 %branch_7_fun.1 = (f32[32,128,256]{2,1,0:T(8,128)S(1)}, f32[14,128,256]{2,1,0:T(8,128)S(1)}) custom-call(s32[16,128]{1,0:T(8,128)S(1)} %get-tuple-element.135.table, f32[32,128,256]{2,1,0:T(8,128)} %get-tuple-element.136.tiles_in, f32[2,32,64,128]{3,2,1,0:T(8,128)} %get-tuple-element.137.panels_in), custom_call_target="tpu_custom_call" | custom-call | tf_op jit(solution)/shard_map/cond/branch_7_fun/pallas_call | solution.py:885
  138.2 2.9 %settle.19 = f32[32,128,256]{2,1,0:T(8,128)} custom-call(s32[16,128]{1,0:T(8,128)S(1)} %get-tuple-element.135.table, f32[32,128,256]{2,1,0:T(8,128)S(1)} %get-tuple-element.138.merged, f32[14,128,256]{2,1,0:T(8,128)S(1)} %get-tuple-element.139.back), custom_call_target="tpu_custom_call" | custom-call | tf_op jit(solution)/shard_map/cond/branch_7_fun/settle/pallas_call | solution.py:837
where the time goes:
time: 142 us
  Pallas kernels  140 us (99%)
    pallas_call x1, Pallas kernels, whole(): pl.pallas_call(functools.partial(whole_kernel, profile, group), in_specs=...  127 us
    pallas_call x1, Pallas kernels, plan(): pl.pallas_call(functools.partial(plan_kernel, profiles), out_shape=[jax.S...  9.93 us
    pallas_call x1, Pallas kernels, settle(): pl.pallas_call(settle_kernel, in_specs=[pl.BlockSpec(memory_space=pltpu.S...  2.94 us

commit v1 on v0

--- a/solution.py
+++ b/solution.py
@@ -304,11 +304,13 @@
 
 
 def plan_kernel(profiles, flags, table, choice, everyone, mine, held, send, recv):
-    count, _, lanes = held.shape
-    diagonals, depth = flags.shape
+    count, lanes = held.shape
+    half = lanes // 2
+    depth = flags.shape[1]
     me = lax.axis_index("row")
     mine[...] = jnp.full(mine.shape, -1, mine.dtype)
-    mine[0:diagonals, 0:depth] = flags[...]
+    for d in range(2):
+        mine[0:1, d * half : d * half + depth] = flags[d : d + 1]
     barrier = pltpu.get_barrier_semaphore()
     mesh_id = pl.DeviceIdType.MESH
     others = [lax.rem(me + by, count) for by in range(1, count)]
@@ -317,10 +319,11 @@
             barrier, inc=1, device_id={"row": other}, device_id_type=mesh_id
         )
     pl.semaphore_wait(barrier, count - 1)
+    here = pl.ds(me, 1)
     copies = [
         pltpu.make_async_remote_copy(
-            src_ref=mine,
-            dst_ref=held.at[me],
+            src_ref=mine.at[pl.ds(0, 1)],
+            dst_ref=held.at[here],
             send_sem=send.at[i],
             recv_sem=recv.at[i],
             device_id={"row": other},
@@ -330,14 +333,20 @@
     ]
     for copy in copies:
         copy.start()
-    held[me] = mine[...]
+    held[here] = mine[0:1]
     for copy in copies:
         copy.wait()
-    everyone[...] = held[...]
+    packed = held[...]
+    everyone[...] = packed
 
     f32 = jnp.float32
     row = lax.broadcasted_iota(jnp.int32, (count, lanes), 0)
-    on = [jnp.where(held[:, d, :] >= 0, 1.0, 0.0) for d in range(2)]
+    lane = lax.broadcasted_iota(jnp.int32, (count, lanes), 1)
+    set_lanes = jnp.where(packed >= 0, 1.0, 0.0)
+    on = [
+        jnp.where(lane < half, x, 0.0)
+        for x in (set_lanes, pltpu.roll(set_lanes, half, axis=1))
+    ]
     after = []
     for x in on:
         under = pltpu.roll(x, count - 1, axis=0)
@@ -476,7 +485,7 @@
     count = lax.axis_size("row")
     lanes = 128
     vmem_spec = pl.BlockSpec(memory_space=pltpu.VMEM)
-    shape = (count, 8, lanes)
+    shape = (count, lanes)
     kind = flags.dtype
     return pl.pallas_call(
         functools.partial(plan_kernel, profiles),
@@ -488,7 +497,7 @@
         in_specs=[vmem_spec],
         out_specs=[vmem_spec, pl.BlockSpec(memory_space=pltpu.SMEM), vmem_spec],
         scratch_shapes=[
-            pltpu.VMEM(shape[1:], kind),
+            pltpu.VMEM((8, lanes), kind),
             pltpu.VMEM(shape, kind),
             pltpu.SemaphoreType.DMA((count - 1,)),
             pltpu.SemaphoreType.DMA((count - 1,)),
@@ -909,7 +918,8 @@
     table, choice, flags = plan(profiles, sweep_group[:, :, 0])
 
     def general(table, flags, tiles, panels):
-        active = flags[:, : sweep_group.shape[0], :depth] >= 0
+        half = flags.shape[1] // 2
+        active = jnp.stack([flags[:, :depth], flags[:, half : half + depth]], axis=1) >= 0
         mine = lax.dynamic_index_in_dim(active, row_index, 0, keepdims=False)
         above = lax.dynamic_index_in_dim(
             active, (row_index + row_count - 1) % row_count, 0, keepdims=False

time: 142 us -> 142 us (level)
  no operation moved by 1% of the time
where the time goes in v1:
time: 142 us; the launch traced here: 141 us
  Pallas kernels  140 us (99%)
    pallas_call x1, Pallas kernels, whole(): pl.pallas_call(functools.partial(whole_kernel, profile, group), in_specs=...  127 us
    pallas_call x1, Pallas kernels, plan(): pl.pallas_call(functools.partial(plan_kernel, profiles), out_shape=[jax.S...  9.87 us
    pallas_call x1, Pallas kernels, settle(): pl.pallas_call(settle_kernel, in_specs=[pl.BlockSpec(memory_space=pltpu.S...  2.94 us

profile of v1, /device:TPU:0, one launch (start us, length us, event | category | flops | bytes accessed | tf_op | source)
XLA Modules:
  0.0 141.4 jit_solution(10167924066163920014)
XLA Ops:
  0.0 9.9 %plan.1 = (s32[16,128]{1,0:T(8,128)S(1)}, s32[1]{0:T(128)}, s32[8,128]{1,0:T(8,128)S(1)}) custom-call(s32[2,32]{1,0:T(2,128)} %bitcast.80), custom_call_target="tpu_custom_call" | custom-call | tf_op jit(solution)/shard_map/plan/pallas_call | solution.py:490
  10.5 130.7 %conditional.1 = (f32[32,1,128,256]{3,2,1,0:T(8,128)}) conditional(s32[]{:T(128)} %bitcast.45, (s32[16,128]{1,0:T(8,128)S(1)}, f32[32,128,256]{2,1,0:T(8,128)}, f32[2,32,64,128]{3,2,1,0:T(8,128)}) %tuple.113, (s32[16,128]{1,0:T(8,128)S(1)}, f32[32,128,256]{2,1,0:T(8,128)}, f32[2,32,64,128]{3,2,1,0:T(8,128)}) %tuple.114, ...), branch_computations={%region_0.0_spmd, %region_1.0_spmd, %region_2.0_spmd, %region_3.0_... | conditional | flops 24273 | bytes 109066552 | solution.py:939
  10.8 127.2 %branch_7_fun.1 = (f32[32,128,256]{2,1,0:T(8,128)S(1)}, f32[14,128,256]{2,1,0:T(8,128)S(1)}) custom-call(s32[16,128]{1,0:T(8,128)S(1)} %get-tuple-element.135.table, f32[32,128,256]{2,1,0:T(8,128)} %get-tuple-element.136.tiles_in, f32[2,32,64,128]{3,2,1,0:T(8,128)} %get-tuple-element.137.panels_in), custom_call_target="tpu_custom_call" | custom-call | tf_op jit(solution)/shard_map/cond/branch_7_fun/pallas_call | solution.py:894
  137.9 2.9 %settle.19 = f32[32,128,256]{2,1,0:T(8,128)} custom-call(s32[16,128]{1,0:T(8,128)S(1)} %get-tuple-element.135.table, f32[32,128,256]{2,1,0:T(8,128)S(1)} %get-tuple-element.138.merged, f32[14,128,256]{2,1,0:T(8,128)S(1)} %get-tuple-element.139.back), custom_call_target="tpu_custom_call" | custom-call | tf_op jit(solution)/shard_map/cond/branch_7_fun/settle/pallas_call | solution.py:846
